TPU v7x, 32 devices: a whole 2x2x4 slice. The times are simulated.
32 devices in a mesh: blk: 16 (over z, y, core), rel: 2 (over x).
Axes of the slice: x: 2, y: 2, z: 4, core: 2. Of those that a mesh axis runs over, the one named last changes fastest.
Arguments:
- source_table: float32 [400, 24576], P(None, ('blk', 'rel')), may hold values from -1.2 to 1.2
- source_state: float32 [24576], P(('blk', 'rel')), may hold values from 0.001 to 0.1
- target_table: float32 [400, 24576], P(None, ('blk', 'rel')), may hold values from -1.2 to 1.2
- target_state: float32 [24576], P(('blk', 'rel')), may hold values from 0.001 to 0.1
- relation_ops: float32 [400, 2048], P(None, 'blk'), may hold values from 0.5 to 1.5
- relation_state: float32 [400, 2048], P(None, 'blk'), may hold values from 0.01 to 1
- source_ids: int32 [2, 16384], P(None, ('blk', 'rel')), may hold values from 0 to 767
- target_ids: int32 [2, 16384], P(None, ('blk', 'rel')), may hold values from 0 to 767
- relation_ids: int32 [2, 16384], P(None, ('blk', 'rel')), may hold values from 0 to 127
- negative_ids: int32 [2, 16384], P(None, ('blk', 'rel')), may hold values from 0 to 767
Outputs:
- new_source: float32 [400, 24576], P(None, ('blk', 'rel'))
- new_source_state: float32 [24576], P(('blk', 'rel'))
- held_target: float32 [400, 24576], P(None, ('blk', 'rel'))
- held_target_state: float32 [24576], P(('blk', 'rel'))
- new_relations: float32 [400, 2048], P(None, 'blk')
- new_relation_state: float32 [400, 2048], P(None, 'blk')
All inputs are finite; a program needn't handle non-finite values.
Results may differ from a plain program's by a relative error of at most 0.0001.
Values sent between devices are 32-bit elements; how exact they have to be, the bound alone decides.
A program may use at most 64 MiB of HBM per device.

v0:
```python
import functools

import jax
import jax.numpy as jnp
from jax import lax
from jax.experimental import pallas as pl
from jax.experimental.pallas import tpu as pltpu
from jax.sharding import PartitionSpec as P

learn_rate = 0.1
epsilon = 1e-06
MESH = pl.DeviceIdType.MESH
F32 = jnp.float32
BF16 = jnp.bfloat16


def split(x):
    high = x.astype(BF16)
    return high, (x - high.astype(F32)).astype(BF16)


def nn(a, b):
    return lax.dot_general(a, b, (((1,), (0,)), ((), ())), preferred_element_type=F32)


def nt(a, b):
    return lax.dot_general(a, b, (((1,), (1,)), ((), ())), preferred_element_type=F32)


def column(row):
    wide = jnp.broadcast_to(row.astype(F32), (8, row.shape[1]))
    return jnp.transpose(wide)[:, :1].astype(jnp.int32)


def emit(*refs):
    inputs, outputs, (first, second, sem) = refs[:6], refs[6:12], refs[12:]
    copies = []
    for i in (0, 2, 4, 5):
        copies.append(pltpu.make_async_copy(inputs[i], outputs[i], sem.at[i]))
        copies[-1].start()
    for i, line in ((1, first), (3, second)):
        line[...] = inputs[i][0, :]
        copies.append(pltpu.make_async_copy(line, outputs[i], sem.at[i]))
        copies[-1].start()
    for copy in copies:
        copy.wait()


def kernel(
    n_blk, n_rel, chunk,
    src_in, srow_in, tgt_in, trow_in, rel_in, rstate_in, sid_in, rid_in, tid_in, nid_in,
    out_src, out_srow, out_tgt, out_trow, out_rel, out_rstate,
    src_ref, srow_ref, tgt_ref, trow_ref, rel_ref, rstate_ref, sid_ref, rid_ref, tid_ref, nid_ref,
    load_sem, hot, rhot, table3, weight_hi, weight_lo, q3t, q_hi, q_lo, picked, relation, gq_ref, counts,
    send, recv, rel_all, send_sem, recv_sem, rsend_sem, rrecv_sem,
):
    loads = {}
    for index, (there, here) in enumerate((
        (sid_in, sid_ref), (rid_in, rid_ref), (tid_in, tid_ref), (nid_in, nid_ref), (rel_in, rel_ref),
        (src_in, src_ref), (trow_in, trow_ref), (tgt_in, tgt_ref), (srow_in, srow_ref), (rstate_in, rstate_ref),
    )):
        loads[index] = pltpu.make_async_copy(there, here, load_sem.at[index])
        loads[index].start()
    dims, rows = src_ref.shape
    buckets, edges = sid_ref.shape
    negs = nid_ref.shape[1]
    rels = rel_ref.shape[1]
    chunks = rows // chunk
    pad = send.shape[2] - dims
    my_blk = lax.axis_index("blk")
    my_rel = lax.axis_index("rel")
    nxt = lax.rem(my_blk + 1, n_blk)
    prv = lax.rem(my_blk + n_blk - 1, n_blk)

    barrier = pltpu.get_barrier_semaphore()
    for other in (nxt, prv):
        pl.semaphore_signal(barrier, inc=1, device_id={"blk": other}, device_id_type=MESH)
    for step in range(1, n_rel):
        pl.semaphore_signal(
            barrier, inc=1, device_id={"rel": lax.rem(my_rel + step, n_rel)}, device_id_type=MESH
        )

    def hop(bucket, c):
        return pltpu.make_async_remote_copy(
            src_ref=send.at[bucket, c],
            dst_ref=recv.at[bucket, c],
            send_sem=send_sem.at[bucket, c],
            recv_sem=recv_sem.at[bucket, c],
            device_id={"blk": nxt},
            device_id_type=MESH,
        )

    for index in range(4):
        loads[index].wait()

    for bucket in range(buckets):
        last = bucket + 1 == buckets
        now_src = src_ref if bucket == 0 else out_src
        sid = sid_ref[pl.ds(bucket, 1), :]
        rid = rid_ref[pl.ds(bucket, 1), :]
        hot[...] = (lax.broadcasted_iota(jnp.int32, (rows, edges), 0) == sid).astype(F32).astype(BF16)
        rhot[...] = (lax.broadcasted_iota(jnp.int32, (rels, edges), 0) == rid).astype(F32).astype(BF16)
        tid = column(tid_ref[pl.ds(bucket, 1), :])
        nid = column(nid_ref[pl.ds(bucket, 1), :])

        for c in range(chunks):
            cols = pl.ds(c * chunk, chunk)
            lane = lax.broadcasted_iota(jnp.int32, (negs, chunk), 1) + c * chunk
            counts[:, cols] = jnp.sum(
                (lane == nid).astype(F32), axis=0, keepdims=True
            ) * (1.0 / negs)

        if bucket == 0:
            for index in range(4, 6):
                loads[index].wait()
        s_hi, s_lo = split(now_src[...])
        picked[...] = nn(s_hi, hot[...]) + nn(s_lo, hot[...])
        r_hi, r_lo = split(rel_ref[...])
        relation[...] = nn(r_hi, rhot[...]) + nn(r_lo, rhot[...])
        queries = picked[...] * relation[...]
        hi, lo = split(queries)
        q_hi[...] = hi
        q_lo[...] = lo
        hi_t = jnp.transpose(hi.astype(F32)).astype(BF16)
        lo_t = jnp.transpose(lo.astype(F32)).astype(BF16)
        q3t[0] = hi_t
        q3t[1] = lo_t
        if bucket == 0:
            for index in range(6, 10):
                loads[index].wait()
        if bucket == 0:
            pl.semaphore_wait(barrier, 2 + n_rel - 1)

        def weigh(c):
            cols = pl.ds(pl.multiple_of(c * chunk, chunk), chunk)
            if bucket == 0:
                table = tgt_ref[:, cols]
            else:
                hop(bucket - 1, c).wait_recv()
                table = recv[bucket - 1, c, :dims, :]
            t_hi, t_lo = split(table)
            if bucket == 0:
                table3[0, c] = t_hi
                table3[1, c] = t_lo
            score = nn(q3t[0], t_hi) + nn(q3t[0], t_lo) + nn(q3t[1], t_hi)
            small = jnp.exp(-jnp.abs(score))
            large = 1.0 / (1.0 + small)
            small = small * large
            up = score >= 0
            sig = jnp.where(up, large, small)
            co = jnp.where(up, small, large)
            lane = lax.broadcasted_iota(jnp.int32, (edges, chunk), 1) + c * chunk
            weight = counts[:, cols] * sig - jnp.where(lane == tid, co, 0.0)
            w_hi, w_lo = split(weight)
            weight_hi[c] = w_hi
            weight_lo[c] = w_lo
            if bucket > 0:
                part = nt(t_hi, w_hi) + nt(t_hi, w_lo) + nt(t_lo, w_hi)
                gq_ref[...] = part if isinstance(c, int) and c == 0 else gq_ref[...] + part

        def finish(c):
            cols = pl.ds(pl.multiple_of(c * chunk, chunk), chunk)
            if bucket == 0:
                table = tgt_ref[:, cols]
                state = trow_ref[cols].reshape(1, chunk)
            else:
                table = recv[bucket - 1, c, :dims, :]
                state = recv[bucket - 1, c, dims:dims + 1, :]
            w_hi = weight_hi[c]
            w_lo = weight_lo[c]
            grad = nn(q_hi[...], w_hi) + nn(q_hi[...], w_lo) + nn(q_lo[...], w_hi)
            fresh = state + jnp.sum(grad * grad, axis=0, keepdims=True) * (1.0 / dims)
            new = table - grad * (learn_rate / (jnp.sqrt(fresh) + epsilon))
            if last:
                out_tgt[:, cols] = new
                out_trow[:, cols] = fresh
            else:
                send[bucket, c, :dims, :] = new
                send[bucket, c, dims:, :] = jnp.broadcast_to(fresh, (pad, chunk))
                hop(bucket, c).start()

        if bucket == 0:

            def both(c, carry):
                weigh(c)
                finish(c)
                return carry

            lax.fori_loop(0, chunks, both, 0)
        else:
            for c in range(chunks):
                weigh(c)
                if not last or c + 1 < chunks:
                    finish(c)
        if bucket == 0:
            grad_query = jnp.zeros((dims, edges), F32)
            for c in range(chunks):
                grad_query += (
                    nt(table3[0, c], weight_hi[c])
                    + nt(table3[0, c], weight_lo[c])
                    + nt(table3[1, c], weight_hi[c])
                )
        else:
            grad_query = gq_ref[...]
        g_hi, g_lo = split(grad_query * picked[...])
        rel_grad = nt(g_hi, rhot[...]) + nt(g_lo, rhot[...])
        if bucket == 0:
            rel_all[my_rel] = rel_grad
        else:
            rel_all[my_rel] = rel_all[my_rel] + rel_grad
        if last:
            for step in range(1, n_rel):
                peer = lax.rem(my_rel + step, n_rel)
                pltpu.make_async_remote_copy(
                    src_ref=rel_all.at[my_rel],
                    dst_ref=rel_all.at[my_rel],
                    send_sem=rsend_sem.at[step - 1],
                    recv_sem=rrecv_sem.at[my_rel],
                    device_id={"rel": peer},
                    device_id_type=MESH,
                ).start()
        if last and bucket > 0:
            finish(chunks - 1)
        g_hi, g_lo = split(grad_query * relation[...])
        src_grad = nt(g_hi, hot[...]) + nt(g_lo, hot[...])
        now_srow = srow_ref[...].reshape(1, rows) if bucket == 0 else out_srow[...]
        fresh = now_srow + jnp.sum(src_grad * src_grad, axis=0, keepdims=True) * (1.0 / dims)
        out_src[...] = now_src[...] - src_grad * (learn_rate / (jnp.sqrt(fresh) + epsilon))
        out_srow[...] = fresh

    for bucket in range(buckets - 1):
        for c in range(chunks):
            hop(bucket, c).wait_send()
    for step in range(1, n_rel):
        peer = lax.rem(my_rel + n_rel - step, n_rel)
        arrived = pltpu.make_async_remote_copy(
            src_ref=rel_all.at[peer],
            dst_ref=rel_all.at[peer],
            send_sem=rsend_sem.at[step - 1],
            recv_sem=rrecv_sem.at[peer],
            device_id={"rel": peer},
            device_id_type=MESH,
        )
        arrived.wait_send()
        arrived.wait_recv()
    total = rel_all[0]
    for step in range(1, n_rel):
        total = total + rel_all[step]
    new_state = rstate_ref[...] + total * total
    out_rstate[...] = new_state
    out_rel[...] = rel_ref[...] - learn_rate * total / (jnp.sqrt(new_state) + epsilon)


def solution(mesh):
    n_blk, n_rel = mesh.shape["blk"], mesh.shape["rel"]

    def per_device(
        source_table, source_state, target_table, target_state, relation_ops, relation_state,
        source_ids, target_ids, relation_ids, negative_ids,
    ):
        dims, rows = source_table.shape
        rels = relation_ops.shape[1]
        buckets, edges = source_ids.shape
        chunk = 256 if rows % 256 == 0 else 128
        chunks = rows // chunk
        vmem = pl.BlockSpec(memory_space=pltpu.VMEM)
        shape = jax.ShapeDtypeStruct
        out = pl.pallas_call(
            functools.partial(kernel, n_blk, n_rel, chunk),
            out_shape=(
                pltpu.VMEM((dims, rows), F32), pltpu.VMEM((1, rows), F32),
                pltpu.VMEM((dims, rows), F32), pltpu.VMEM((1, rows), F32),
                pltpu.VMEM((dims, rels), F32), pltpu.VMEM((dims, rels), F32),
            ),
            in_specs=[pl.BlockSpec(memory_space=pltpu.HBM)] * 10,
            out_specs=(vmem,) * 6,
            scratch_shapes=[
                pltpu.VMEM((dims, rows), F32), pltpu.VMEM((rows,), F32),
                pltpu.VMEM((dims, rows), F32), pltpu.VMEM((rows,), F32),
                pltpu.VMEM((dims, rels), F32), pltpu.VMEM((dims, rels), F32),
                *[pltpu.VMEM(ids.shape, jnp.int32) for ids in (source_ids, relation_ids, target_ids, negative_ids)],
                pltpu.SemaphoreType.DMA((10,)),
                pltpu.VMEM((rows, edges), BF16),
                pltpu.VMEM((rels, edges), BF16),
                pltpu.VMEM((2, chunks, dims, chunk), BF16),
                pltpu.VMEM((chunks, edges, chunk), BF16),
                pltpu.VMEM((chunks, edges, chunk), BF16),
                pltpu.VMEM((2, edges, dims), BF16),
                pltpu.VMEM((dims, edges), BF16),
                pltpu.VMEM((dims, edges), BF16),
                pltpu.VMEM((dims, edges), F32),
                pltpu.VMEM((dims, edges), F32),
                pltpu.VMEM((dims, edges), F32),
                pltpu.VMEM((1, rows), F32),
                pltpu.VMEM((buckets - 1, chunks, dims + 8, chunk), F32),
                pltpu.VMEM((buckets - 1, chunks, dims + 8, chunk), F32),
                pltpu.VMEM((n_rel, dims, rels), F32),
                pltpu.SemaphoreType.DMA((buckets - 1, chunks)),
                pltpu.SemaphoreType.DMA((buckets - 1, chunks)),
                pltpu.SemaphoreType.DMA((n_rel,)),
                pltpu.SemaphoreType.DMA((n_rel,)),
            ],
            compiler_params=pltpu.CompilerParams(
                collective_id=0, has_side_effects=True, vmem_limit_bytes=40 * 1024 * 1024
            ),
        )(*(
            pltpu.with_memory_space_constraint(x, pltpu.HBM) for x in (
                source_table, source_state, target_table, target_state,
                relation_ops, relation_state, source_ids, relation_ids,
                target_ids, negative_ids,
            )
        ))
        hbm = pl.BlockSpec(memory_space=pl.ANY)
        return pl.pallas_call(
            emit,
            out_shape=(
                shape((dims, rows), F32), shape((rows,), F32),
                shape((dims, rows), F32), shape((rows,), F32),
                shape((dims, rels), F32), shape((dims, rels), F32),
            ),
            in_specs=[vmem] * 6,
            out_specs=(hbm,) * 6,
            scratch_shapes=[pltpu.VMEM((rows,), F32), pltpu.VMEM((rows,), F32), pltpu.SemaphoreType.DMA((6,))],
            compiler_params=pltpu.CompilerParams(vmem_limit_bytes=16 * 1024 * 1024),
        )(*out)

    split_both = ("blk", "rel")
    return jax.shard_map(
        per_device,
        mesh=mesh,
        in_specs=(
            P(None, split_both), P(split_both), P(None, split_both), P(split_both),
            P(None, "blk"), P(None, "blk"),
            P(None, split_both), P(None, split_both), P(None, split_both), P(None, split_both),
        ),
        out_specs=(
            P(None, split_both), P(split_both), P(None, split_both), P(split_both),
            P(None, "blk"), P(None, "blk"),
        ),
        check_vma=False,
    )
```

profile of v0, /device:TPU:0, one launch (start us, length us, event | category | flops | bytes accessed | tf_op | source)
XLA Modules:
  0.0 34.8 jit_solution(3931871178875734308)
XLA Ops:
  0.6 32.6 %shard_map.145 = (f32[400,768]{1,0:T(8,128)S(1)}, f32[1,768]{1,0:T(1,128)S(1)}, f32[400,768]{1,0:T(8,128)S(1)}, f32[1,768]{1,0:T(1,128)S(1)}, f32[400,128]{1,0:T(8,128)S(1)}, /*index=5*/f32[400,128]{1,0:T(8,128)S(1)}) custom-call(f32[400,768]{1,0:T(8,128)} %src_in.1, f32[768]{0:T(1024)} %srow_in.1, f32[400,768]{1,0:T(8,128)} %tgt_in.1, f32[768]{0:T(1024)} %trow_in.1, ...), custom_call_target="tpu_custom_call" | custom-call | tf_op jit(solution)/shard_map/pallas_call | solution.py:268
  33.2 1.6 %shard_map.146 = (f32[400,768]{1,0:T(8,128)}, f32[768]{0:T(1024)}, f32[400,768]{1,0:T(8,128)}, f32[768]{0:T(1024)}, f32[400,128]{1,0:T(8,128)}, /*index=5*/f32[400,128]{1,0:T(8,128)}) custom-call(f32[400,768]{1,0:T(8,128)S(1)} %get-tuple-element.12.refs_0_, f32[1,768]{1,0:T(1,128)S(1)} %get-tuple-element.13.refs_1_, ...), custom_call_target="tpu_custom_call" | custom-call | tf_op jit(solution)/shard_map/pallas_call | solution.py:314
where the time goes:
time: 35 us; the launch traced here: 34.8 us
  Pallas kernels  34.2 us (98%)
  between operations  0.64 us (2%)
    pallas_call x1, Pallas kernels, per_device(): pl.pallas_call(functools.partial(kernel, n_blk, n_rel, chunk), out_shape=...  32.6 us
    pallas_call x1, Pallas kernels, per_device(): pl.pallas_call(emit, out_shape=(shape((dims, rows), F32), shape((rows,),...  1.62 us

commit v1 on v0

v1 whole, which is shorter than its diff:
```python
import functools

import jax
import jax.numpy as jnp
from jax import lax
from jax.experimental import pallas as pl
from jax.experimental.pallas import tpu as pltpu
from jax.sharding import PartitionSpec as P

learn_rate = 0.1
epsilon = 1e-06
LANES = 128
MESH = pl.DeviceIdType.MESH
F32 = jnp.float32
BF16 = jnp.bfloat16


def split(x):
    high = x.astype(BF16)
    return high, (x - high.astype(F32)).astype(BF16)


def nn(a, b):
    return lax.dot_general(a, b, (((1,), (0,)), ((), ())), preferred_element_type=F32)


def nt(a, b):
    return lax.dot_general(a, b, (((1,), (1,)), ((), ())), preferred_element_type=F32)


def column(row):
    wide = jnp.broadcast_to(row.astype(F32), (8, row.shape[1]))
    return jnp.transpose(wide)[:, :1].astype(jnp.int32)


def chunk_plan(rows):
    if rows % 256 == 0 and rows >= 512:
        widths = [LANES] + [256] * (rows // 256 - 1) + [LANES]
    else:
        widths = [LANES] * (rows // LANES)
    return [(sum(widths[:i]), w) for i, w in enumerate(widths)]


def row_blocks(dims):
    half = (dims // 2 + 15) // 16 * 16
    return [(0, half), (half, dims - half)]


def emit(*refs):
    inputs, outputs, (first, second, sem) = refs[:6], refs[6:12], refs[12:]
    copies = []
    for i in (0, 2, 4, 5):
        copies.append(pltpu.make_async_copy(inputs[i], outputs[i], sem.at[i]))
        copies[-1].start()
    for i, line in ((1, first), (3, second)):
        line[...] = inputs[i][0, :]
        copies.append(pltpu.make_async_copy(line, outputs[i], sem.at[i]))
        copies[-1].start()
    for copy in copies:
        copy.wait()


def kernel(n_blk, n_rel, plan, blocks, *refs):
    refs = list(refs)

    def take(n):
        out = refs[:n]
        del refs[:n]
        return out

    src_in, srow_in, tgt_in, trow_in, rel_in, rstate_in, sid_in, rid_in, tid_in, nid_in = take(10)
    out_src, out_srow, out_tgt, out_trow, out_rel, out_rstate = take(6)
    src_ref, srow_ref, tgt_ref, trow_ref, rel_ref, rstate_ref, sid_ref, rid_ref, tid_ref, nid_ref = take(10)
    load_sem, hot, rhot, qt_ref, q_ref, picked, relation, gq_ref, rel_all = take(9)
    rsend_sem, rrecv_sem, send_sem, recv_sem, row_send, row_recv = take(6)
    tables, weights = take(len(plan)), take(len(plan))
    send, recv = take(len(plan)), take(len(plan))
    dims, rows = src_ref.shape
    buckets, edges = sid_ref.shape
    negs = nid_ref.shape[1]
    rels = rel_ref.shape[1]
    final = len(plan) - 1
    my_blk = lax.axis_index("blk")
    my_rel = lax.axis_index("rel")
    nxt = lax.rem(my_blk + 1, n_blk)
    prv = lax.rem(my_blk + n_blk - 1, n_blk)

    loads = []

    def load(there, here):
        loads.append(pltpu.make_async_copy(there, here, load_sem.at[len(loads)]))
        loads[-1].start()
        return loads[-1]

    load_ids = [load(sid_in, sid_ref), load(rid_in, rid_ref)]
    load_rel = load(rel_in, rel_ref)
    load_src = [load(src_in.at[pl.ds(r, n)], src_ref.at[pl.ds(r, n)]) for r, n in blocks]
    load_other = [load(tid_in, tid_ref), load(nid_in, nid_ref), load(trow_in, trow_ref)]
    load_tgt = load(tgt_in, tgt_ref)
    load_late = [load(srow_in, srow_ref), load(rstate_in, rstate_ref)]

    barrier = pltpu.get_barrier_semaphore()
    pl.semaphore_signal(barrier, inc=1, device_id={"blk": prv}, device_id_type=MESH)
    for step in range(1, n_rel):
        pl.semaphore_signal(
            barrier, inc=1, device_id={"rel": lax.rem(my_rel + step, n_rel)}, device_id_type=MESH
        )

    def hop(bucket, c):
        return pltpu.make_async_remote_copy(
            src_ref=send[c].at[bucket],
            dst_ref=recv[c].at[bucket],
            send_sem=send_sem.at[0, bucket, c],
            recv_sem=recv_sem.at[0, bucket, c],
            device_id={"blk": nxt},
            device_id_type=MESH,
        )

    def row_hop(bucket, c):
        return pltpu.make_async_remote_copy(
            src_ref=row_send.at[bucket, c, :, pl.ds(0, plan[c][1])],
            dst_ref=row_recv.at[bucket, c, :, pl.ds(0, plan[c][1])],
            send_sem=send_sem.at[1, bucket, c],
            recv_sem=recv_sem.at[1, bucket, c],
            device_id={"blk": nxt},
            device_id_type=MESH,
        )

    def rel_hop(to, slot, step, b):
        r, n = blocks[b]
        return pltpu.make_async_remote_copy(
            src_ref=rel_all.at[slot, pl.ds(r, n)],
            dst_ref=rel_all.at[slot, pl.ds(r, n)],
            send_sem=rsend_sem.at[step - 1, b],
            recv_sem=rrecv_sem.at[slot, b],
            device_id={"rel": to},
            device_id_type=MESH,
        )

    def put_pair(ref, hi, lo, twice):
        width = hi.shape[1]
        if width == LANES:
            ref[0, :, :LANES] = hi
            ref[0, :, LANES:] = lo
            if twice:
                ref[1, :, :LANES] = hi
                ref[1, :, LANES:] = hi
        else:
            ref[0] = hi
            ref[1] = lo

    def fold(wide):
        return wide[:, :LANES] + wide[:, LANES:]

    for copy in load_ids:
        copy.wait()

    for bucket in range(buckets):
        last = bucket + 1 == buckets
        now_src = src_ref if bucket == 0 else out_src
        sid = sid_ref[pl.ds(bucket, 1), :]
        rid = rid_ref[pl.ds(bucket, 1), :]
        rhot[...] = (lax.broadcasted_iota(jnp.int32, (rels, edges), 0) == rid).astype(F32).astype(BF16)
        hot[...] = (lax.broadcasted_iota(jnp.int32, (rows, edges), 0) == sid).astype(F32).astype(BF16)
        if bucket == 0:
            load_rel.wait()
        r_hi, r_lo = split(rel_ref[...])
        relation[...] = nn(r_hi, rhot[...]) + nn(r_lo, rhot[...])
        asked = []
        for b, (r, n) in enumerate(blocks):
            part = pl.ds(r, n)
            if bucket == 0:
                load_src[b].wait()
            s_hi, s_lo = split(now_src[part, :])
            got = nn(s_hi, hot[...]) + nn(s_lo, hot[...])
            picked[part, :] = got
            queries = got * relation[part, :]
            hi, lo = split(queries)
            q_ref[0, part, :] = hi
            q_ref[1, part, :] = lo
            asked.append(queries)
        hi, lo = split(jnp.transpose(jnp.concatenate(asked, axis=0)))
        qt_ref[0] = hi
        qt_ref[1] = lo

        if bucket == 0:
            for copy in load_other:
                copy.wait()
        tid = column(tid_ref[pl.ds(bucket, 1), :])
        nid = column(nid_ref[pl.ds(bucket, 1), :])

        def weigh(c):
            start, width = plan[c]
            cols = pl.ds(start, width)
            lane = lax.broadcasted_iota(jnp.int32, (negs, width), 1) + start
            count = jnp.sum((lane == nid).astype(F32), axis=0, keepdims=True) * (1.0 / negs)
            if bucket == 0:
                table = tgt_ref[:, cols]
            else:
                hop(bucket - 1, c).wait_recv()
                table = recv[c][bucket - 1]
            t_hi, t_lo = split(table)
            put_pair(tables[c], t_hi, t_lo, True)
            if width == LANES:
                score = fold(nn(qt_ref[0], tables[c][0])) + nn(qt_ref[1], t_hi)
            else:
                score = nn(qt_ref[0], t_hi) + nn(qt_ref[0], t_lo) + nn(qt_ref[1], t_hi)
            small = jnp.exp(-jnp.abs(score))
            large = 1.0 / (1.0 + small)
            small = small * large
            up = score >= 0
            sig = jnp.where(up, large, small)
            co = jnp.where(up, small, large)
            lane = lax.broadcasted_iota(jnp.int32, (edges, width), 1) + start
            weight = count * sig - jnp.where(lane == tid, co, 0.0)
            w_hi, w_lo = split(weight)
            put_pair(weights[c], w_hi, w_lo, False)

        def query_part(c, part):
            if plan[c][1] == LANES:
                return (
                    nt(tables[c][1, part, :], weights[c][0])
                    + nt(tables[c][0, part, LANES:], weights[c][0, :, :LANES])
                )
            return (
                nt(tables[c][0, part, :], weights[c][0])
                + nt(tables[c][0, part, :], weights[c][1])
                + nt(tables[c][1, part, :], weights[c][0])
            )

        def finish(c):
            start, width = plan[c]
            cols = pl.ds(start, width)
            if bucket == 0:
                table = tgt_ref[:, cols]
                state = trow_ref[cols].reshape(1, width)
            else:
                row_hop(bucket - 1, c).wait_recv()
                table = recv[c][bucket - 1]
                state = row_recv[bucket - 1, c, :, :width]
            if width == LANES:
                grad = fold(nn(q_ref[0], weights[c][0])) + nn(q_ref[1], weights[c][0, :, :LANES])
            else:
                grad = nn(q_ref[0], weights[c][0]) + nn(q_ref[0], weights[c][1]) + nn(q_ref[1], weights[c][0])
            fresh = state + jnp.sum(grad * grad, axis=0, keepdims=True) * (1.0 / dims)
            new = table - grad * (learn_rate / (jnp.sqrt(fresh) + epsilon))
            if last:
                out_tgt[:, cols] = new
                out_trow[:, cols] = fresh
            else:
                send[c][bucket] = new
                row_send[bucket, c, :, :width] = fresh
                hop(bucket, c).start()
                row_hop(bucket, c).start()

        def relate(part, whole):
            g_hi, g_lo = split(whole * picked[part, :])
            rel_grad = nt(g_hi, rhot[...]) + nt(g_lo, rhot[...])
            if bucket == 0:
                rel_all[my_rel, part, :] = rel_grad
            else:
                rel_all[my_rel, part, :] = rel_all[my_rel, part, :] + rel_grad

        if bucket == 0:
            load_tgt.wait()
            for copy in load_late:
                copy.wait()
            pl.semaphore_wait(barrier, n_rel)
        everything = pl.ds(0, dims)
        if not last:
            for c in range(len(plan)):
                weigh(c)
                finish(c)
            total = query_part(0, everything)
            for c in range(1, len(plan)):
                total += query_part(c, everything)
            gq_ref[...] = total
            relate(everything, total)
        else:
            for c in range(final):
                weigh(c)
                part = query_part(c, everything)
                gq_ref[...] = part if c == 0 else gq_ref[...] + part
                finish(c)
            weigh(final)
            for b, (r, n) in enumerate(blocks):
                part = pl.ds(r, n)
                whole = query_part(final, part)
                if final > 0:
                    whole = gq_ref[part, :] + whole
                gq_ref[part, :] = whole
                relate(part, whole)
                for step in range(1, n_rel):
                    rel_hop(lax.rem(my_rel + step, n_rel), my_rel, step, b).start()
            finish(final)
        g_hi, g_lo = split(gq_ref[...] * relation[...])
        src_grad = nt(g_hi, hot[...]) + nt(g_lo, hot[...])
        now_srow = srow_ref[...].reshape(1, rows) if bucket == 0 else out_srow[...]
        fresh = now_srow + jnp.sum(src_grad * src_grad, axis=0, keepdims=True) * (1.0 / dims)
        out_src[...] = now_src[...] - src_grad * (learn_rate / (jnp.sqrt(fresh) + epsilon))
        out_srow[...] = fresh

    for bucket in range(buckets - 1):
        for c in range(len(plan)):
            hop(bucket, c).wait_send()
            row_hop(bucket, c).wait_send()
    for b, (r, n) in enumerate(blocks):
        part = pl.ds(r, n)
        for step in range(1, n_rel):
            peer = lax.rem(my_rel + n_rel - step, n_rel)
            arrived = rel_hop(peer, peer, step, b)
            arrived.wait_send()
            arrived.wait_recv()
        total = rel_all[0, part, :]
        for step in range(1, n_rel):
            total = total + rel_all[step, part, :]
        new_state = rstate_ref[part, :] + total * total
        out_rstate[part, :] = new_state
        out_rel[part, :] = rel_ref[part, :] - learn_rate * total / (jnp.sqrt(new_state) + epsilon)


def solution(mesh):
    n_blk, n_rel = mesh.shape["blk"], mesh.shape["rel"]

    def per_device(
        source_table, source_state, target_table, target_state, relation_ops, relation_state,
        source_ids, target_ids, relation_ids, negative_ids,
    ):
        dims, rows = source_table.shape
        rels = relation_ops.shape[1]
        buckets, edges = source_ids.shape
        plan = chunk_plan(rows)
        blocks = row_blocks(dims)
        chunks = len(plan)
        vmem = pl.BlockSpec(memory_space=pltpu.VMEM)
        shape = jax.ShapeDtypeStruct
        moves = [pltpu.VMEM((buckets - 1, dims, width), F32) for _, width in plan]
        out = pl.pallas_call(
            functools.partial(kernel, n_blk, n_rel, plan, blocks),
            out_shape=(
                pltpu.VMEM((dims, rows), F32), pltpu.VMEM((1, rows), F32),
                pltpu.VMEM((dims, rows), F32), pltpu.VMEM((1, rows), F32),
                pltpu.VMEM((dims, rels), F32), pltpu.VMEM((dims, rels), F32),
            ),
            in_specs=[pl.BlockSpec(memory_space=pltpu.HBM)] * 10,
            out_specs=(vmem,) * 6,
            scratch_shapes=[
                pltpu.VMEM((dims, rows), F32), pltpu.VMEM((rows,), F32),
                pltpu.VMEM((dims, rows), F32), pltpu.VMEM((rows,), F32),
                pltpu.VMEM((dims, rels), F32), pltpu.VMEM((dims, rels), F32),
                *[pltpu.VMEM(ids.shape, jnp.int32) for ids in (source_ids, relation_ids, target_ids, negative_ids)],
                pltpu.SemaphoreType.DMA((9 + len(blocks),)),
                pltpu.VMEM((rows, edges), BF16),
                pltpu.VMEM((rels, edges), BF16),
                pltpu.VMEM((2, edges, dims), BF16),
                pltpu.VMEM((2, dims, edges), BF16),
                pltpu.VMEM((dims, edges), F32),
                pltpu.VMEM((dims, edges), F32),
                pltpu.VMEM((dims, edges), F32),
                pltpu.VMEM((n_rel, dims, rels), F32),
                pltpu.SemaphoreType.DMA((n_rel, len(blocks))),
                pltpu.SemaphoreType.DMA((n_rel, len(blocks))),
                pltpu.SemaphoreType.DMA((2, buckets - 1, chunks)),
                pltpu.SemaphoreType.DMA((2, buckets - 1, chunks)),
                pltpu.VMEM((buckets - 1, chunks, 1, 256), F32),
                pltpu.VMEM((buckets - 1, chunks, 1, 256), F32),
                *[pltpu.VMEM((2, dims, 256), BF16) for _ in plan],
                *[pltpu.VMEM((2, edges, 256), BF16) for _ in plan],
                *moves,
                *moves,
            ],
            compiler_params=pltpu.CompilerParams(
                collective_id=0, has_side_effects=True, vmem_limit_bytes=40 * 1024 * 1024
            ),
        )(*(
            pltpu.with_memory_space_constraint(x, pltpu.HBM) for x in (
                source_table, source_state, target_table, target_state,
                relation_ops, relation_state, source_ids, relation_ids,
                target_ids, negative_ids,
            )
        ))
        hbm = pl.BlockSpec(memory_space=pl.ANY)
        return pl.pallas_call(
            emit,
            out_shape=(
                shape((dims, rows), F32), shape((rows,), F32),
                shape((dims, rows), F32), shape((rows,), F32),
                shape((dims, rels), F32), shape((dims, rels), F32),
            ),
            in_specs=[vmem] * 6,
            out_specs=(hbm,) * 6,
            scratch_shapes=[pltpu.VMEM((rows,), F32), pltpu.VMEM((rows,), F32), pltpu.SemaphoreType.DMA((6,))],
            compiler_params=pltpu.CompilerParams(vmem_limit_bytes=16 * 1024 * 1024),
        )(*out)

    split_both = ("blk", "rel")
    return jax.shard_map(
        per_device,
        mesh=mesh,
        in_specs=(
            P(None, split_both), P(split_both), P(None, split_both), P(split_both),
            P(None, "blk"), P(None, "blk"),
            P(None, split_both), P(None, split_both), P(None, split_both), P(None, split_both),
        ),
        out_specs=(
            P(None, split_both), P(split_both), P(None, split_both), P(split_both),
            P(None, "blk"), P(None, "blk"),
        ),
        check_vma=False,
    )
```

time: 35 us -> 33.1 us (0.946)
  Pallas kernels: 34.2 us -> 32.3 us
    pallas_call x1, Pallas kernels: 32.6 us -> 30.7 us  [per_device(): pl.pallas_call(functools.partial(kernel, n_blk, n_rel, plan, blocks), out...]
where the time goes in v1:
time: 33.1 us; the launch traced here: 32.9 us
  Pallas kernels  32.3 us (98%)
  between operations  0.64 us (2%)
    pallas_call x1, Pallas kernels, per_device(): pl.pallas_call(functools.partial(kernel, n_blk, n_rel, plan, blocks), out...  30.7 us
    pallas_call x1, Pallas kernels, per_device(): pl.pallas_call(emit, out_shape=(shape((dims, rows), F32), shape((rows,),...  1.62 us

profile of v1, /device:TPU:0, one launch (start us, length us, event | category | flops | bytes accessed | tf_op | source)
XLA Modules:
  0.0 32.9 jit_solution(7905174346460223742)
XLA Ops:
  0.6 30.7 %shard_map.145 = (f32[400,768]{1,0:T(8,128)S(1)}, f32[1,768]{1,0:T(1,128)S(1)}, f32[400,768]{1,0:T(8,128)S(1)}, f32[1,768]{1,0:T(1,128)S(1)}, f32[400,128]{1,0:T(8,128)S(1)}, /*index=5*/f32[400,128]{1,0:T(8,128)S(1)}) custom-call(f32[400,768]{1,0:T(8,128)} %refs_0_.1, f32[768]{0:T(1024)} %refs_1_.1, f32[400,768]{1,0:T(8,128)} %refs_2_.1, f32[768]{0:T(1024)} %refs_3_.1, ...), custom_call_target="tpu_custom_call" | custom-call | tf_op jit(solution)/shard_map/pallas_call | solution.py:338
  31.3 1.6 %shard_map.146 = (f32[400,768]{1,0:T(8,128)}, f32[768]{0:T(1024)}, f32[400,768]{1,0:T(8,128)}, f32[768]{0:T(1024)}, f32[400,128]{1,0:T(8,128)}, /*index=5*/f32[400,128]{1,0:T(8,128)}) custom-call(f32[400,768]{1,0:T(8,128)S(1)} %get-tuple-element.12.refs_0_, f32[1,768]{1,0:T(1,128)S(1)} %get-tuple-element.13.refs_1_, ...), custom_call_target="tpu_custom_call" | custom-call | tf_op jit(solution)/shard_map/pallas_call | solution.py:383

commit v2 on v1

--- a/solution.py
+++ b/solution.py
@@ -33,6 +33,18 @@
     return jnp.transpose(wide)[:, :1].astype(jnp.int32)
 
 
+def one_hot(row, height):
+    low = lax.rem(row, LANES)
+    inner = (lax.broadcasted_iota(jnp.int32, (LANES, row.shape[1]), 0) == low).astype(F32).astype(BF16)
+    if height == LANES:
+        return inner
+    out = []
+    for start in range(0, height, LANES):
+        here = (row - low == start).astype(F32).astype(BF16)
+        out.append(inner * jnp.broadcast_to(here, inner.shape))
+    return jnp.concatenate(out, axis=0)
+
+
 def chunk_plan(rows):
     if rows % 256 == 0 and rows >= 512:
         widths = [LANES] + [256] * (rows // 256 - 1) + [LANES]
@@ -42,8 +54,24 @@
 
 
 def row_blocks(dims):
+    first = min(256, dims // 16 * 16)
     half = (dims // 2 + 15) // 16 * 16
-    return [(0, half), (half, dims - half)]
+    return [(0, first), (first, dims - first)], [(0, half), (half, dims - half)]
+
+
+def lane_gather(table, index):
+    tall = table.shape[0]
+    groups = table.shape[1] // LANES
+    out = []
+    for start in range(0, index.shape[1], LANES):
+        one = jnp.broadcast_to(index[:, start:start + LANES], (tall, LANES))
+        low = lax.rem(one, LANES)
+        got = jnp.take_along_axis(table[:, :LANES], low, axis=1)
+        for g in range(1, groups):
+            other = jnp.take_along_axis(table[:, g * LANES:(g + 1) * LANES], low, axis=1)
+            got = jnp.where(one >= g * LANES, other, got)
+        out.append(got)
+    return jnp.concatenate(out, axis=1)
 
 
 def emit(*refs):
@@ -60,7 +88,7 @@
         copy.wait()
 
 
-def kernel(n_blk, n_rel, plan, blocks, *refs):
+def kernel(n_blk, n_rel, plan, arrivals, blocks, *refs):
     refs = list(refs)
 
     def take(n):
@@ -71,7 +99,7 @@
     src_in, srow_in, tgt_in, trow_in, rel_in, rstate_in, sid_in, rid_in, tid_in, nid_in = take(10)
     out_src, out_srow, out_tgt, out_trow, out_rel, out_rstate = take(6)
     src_ref, srow_ref, tgt_ref, trow_ref, rel_ref, rstate_ref, sid_ref, rid_ref, tid_ref, nid_ref = take(10)
-    load_sem, hot, rhot, qt_ref, q_ref, picked, relation, gq_ref, rel_all = take(9)
+    load_sem, hot, rhot, qt_ref, q_ref, picked, relation, gq_ref, counts, rel_all = take(10)
     rsend_sem, rrecv_sem, send_sem, recv_sem, row_send, row_recv = take(6)
     tables, weights = take(len(plan)), take(len(plan))
     send, recv = take(len(plan)), take(len(plan))
@@ -80,6 +108,7 @@
     negs = nid_ref.shape[1]
     rels = rel_ref.shape[1]
     final = len(plan) - 1
+    groups = [(e, min(256, edges - e)) for e in range(0, edges, 256)]
     my_blk = lax.axis_index("blk")
     my_rel = lax.axis_index("rel")
     nxt = lax.rem(my_blk + 1, n_blk)
@@ -92,12 +121,16 @@
         loads[-1].start()
         return loads[-1]
 
-    load_ids = [load(sid_in, sid_ref), load(rid_in, rid_ref)]
+    load_ids = [
+        load(sid_in, sid_ref), load(rid_in, rid_ref), load(nid_in, nid_ref), load(tid_in, tid_ref)
+    ]
     load_rel = load(rel_in, rel_ref)
-    load_src = [load(src_in.at[pl.ds(r, n)], src_ref.at[pl.ds(r, n)]) for r, n in blocks]
-    load_other = [load(tid_in, tid_ref), load(nid_in, nid_ref), load(trow_in, trow_ref)]
-    load_tgt = load(tgt_in, tgt_ref)
-    load_late = [load(srow_in, srow_ref), load(rstate_in, rstate_ref)]
+    load_src = [load(src_in.at[pl.ds(r, n)], src_ref.at[pl.ds(r, n)]) for r, n in arrivals]
+    load_tgt = [
+        load(tgt_in.at[:, pl.ds(start, width)], tgt_ref.at[:, pl.ds(start, width)])
+        for start, width in ((0, plan[0][1]), (plan[0][1], rows - plan[0][1])) if width
+    ]
+    load_late = [load(trow_in, trow_ref), load(srow_in, srow_ref), load(rstate_in, rstate_ref)]
 
     barrier = pltpu.get_barrier_semaphore()
     pl.semaphore_signal(barrier, inc=1, device_id={"blk": prv}, device_id_type=MESH)
@@ -137,17 +170,17 @@
             device_id_type=MESH,
         )
 
-    def put_pair(ref, hi, lo, twice):
+    def put_pair(ref, hi, lo, twice, part=slice(None)):
         width = hi.shape[1]
         if width == LANES:
-            ref[0, :, :LANES] = hi
-            ref[0, :, LANES:] = lo
+            ref[0, part, :LANES] = hi
+            ref[0, part, LANES:] = lo
             if twice:
                 ref[1, :, :LANES] = hi
                 ref[1, :, LANES:] = hi
         else:
-            ref[0] = hi
-            ref[1] = lo
+            ref[0, part, :] = hi
+            ref[1, part, :] = lo
 
     def fold(wide):
         return wide[:, :LANES] + wide[:, LANES:]
@@ -160,61 +193,55 @@
         now_src = src_ref if bucket == 0 else out_src
         sid = sid_ref[pl.ds(bucket, 1), :]
         rid = rid_ref[pl.ds(bucket, 1), :]
-        rhot[...] = (lax.broadcasted_iota(jnp.int32, (rels, edges), 0) == rid).astype(F32).astype(BF16)
-        hot[...] = (lax.broadcasted_iota(jnp.int32, (rows, edges), 0) == sid).astype(F32).astype(BF16)
         if bucket == 0:
             load_rel.wait()
-        r_hi, r_lo = split(rel_ref[...])
-        relation[...] = nn(r_hi, rhot[...]) + nn(r_lo, rhot[...])
-        asked = []
-        for b, (r, n) in enumerate(blocks):
-            part = pl.ds(r, n)
-            if bucket == 0:
-                load_src[b].wait()
-            s_hi, s_lo = split(now_src[part, :])
-            got = nn(s_hi, hot[...]) + nn(s_lo, hot[...])
-            picked[part, :] = got
-            queries = got * relation[part, :]
+        hot[...] = one_hot(sid, rows)
+        nid = column(nid_ref[pl.ds(bucket, 1), :])
+        tid = column(tid_ref[pl.ds(bucket, 1), :])
+        for start in range(0, rows, LANES):
+            lane = lax.broadcasted_iota(jnp.int32, (negs, LANES), 1) + start
+            counts[:, pl.ds(start, LANES)] = jnp.sum(
+                (lane == nid).astype(F32), axis=0, keepdims=True
+            ) * (0.5 / negs)
+        relation[...] = lane_gather(rel_ref[...], rid)
+        if bucket == 0:
+            for copy in load_src + load_tgt[:1]:
+                copy.wait()
+        s_hi, s_lo = split(now_src[...])
+        for e, m in groups:
+            some = pl.ds(e, m)
+            picked[:, some] = nn(s_hi, hot[:, some]) + nn(s_lo, hot[:, some])
+        for e, m in groups:
+            some = pl.ds(e, m)
+            queries = picked[:, some] * relation[:, some]
+            hi, lo = split(jnp.transpose(queries * 0.5))
+            qt_ref[0, some, :] = hi
+            qt_ref[1, some, :] = lo
             hi, lo = split(queries)
-            q_ref[0, part, :] = hi
-            q_ref[1, part, :] = lo
-            asked.append(queries)
-        hi, lo = split(jnp.transpose(jnp.concatenate(asked, axis=0)))
-        qt_ref[0] = hi
-        qt_ref[1] = lo
-
-        if bucket == 0:
-            for copy in load_other:
-                copy.wait()
-        tid = column(tid_ref[pl.ds(bucket, 1), :])
-        nid = column(nid_ref[pl.ds(bucket, 1), :])
+            q_ref[0, :, some] = hi
+            q_ref[1, :, some] = lo
+        rhot[...] = one_hot(rid, rels)
 
         def weigh(c):
             start, width = plan[c]
             cols = pl.ds(start, width)
-            lane = lax.broadcasted_iota(jnp.int32, (negs, width), 1) + start
-            count = jnp.sum((lane == nid).astype(F32), axis=0, keepdims=True) * (1.0 / negs)
-            if bucket == 0:
-                table = tgt_ref[:, cols]
-            else:
-                hop(bucket - 1, c).wait_recv()
-                table = recv[c][bucket - 1]
+            table = tgt_ref[:, cols] if bucket == 0 else recv[c][bucket - 1]
             t_hi, t_lo = split(table)
             put_pair(tables[c], t_hi, t_lo, True)
-            if width == LANES:
-                score = fold(nn(qt_ref[0], tables[c][0])) + nn(qt_ref[1], t_hi)
-            else:
-                score = nn(qt_ref[0], t_hi) + nn(qt_ref[0], t_lo) + nn(qt_ref[1], t_hi)
-            small = jnp.exp(-jnp.abs(score))
-            large = 1.0 / (1.0 + small)
-            small = small * large
-            up = score >= 0
-            sig = jnp.where(up, large, small)
-            co = jnp.where(up, small, large)
-            lane = lax.broadcasted_iota(jnp.int32, (edges, width), 1) + start
-            weight = count * sig - jnp.where(lane == tid, co, 0.0)
-            w_hi, w_lo = split(weight)
-            put_pair(weights[c], w_hi, w_lo, False)
+            count = counts[:, cols]
+            lane = lax.broadcasted_iota(jnp.int32, (edges // len(groups), width), 1) + start
+            for e, m in groups:
+                some = pl.ds(e, m)
+                if width == LANES:
+                    score = fold(nn(qt_ref[0, some, :], tables[c][0])) + nn(qt_ref[1, some, :], t_hi)
+                else:
+                    score = (
+                        nn(qt_ref[0, some, :], t_hi) + nn(qt_ref[0, some, :], t_lo) + nn(qt_ref[1, some, :], t_hi)
+                    )
+                half = jnp.tanh(score)
+                weight = count * half + count - jnp.where(lane == tid[e:e + m], 0.5 - 0.5 * half, 0.0)
+                w_hi, w_lo = split(weight)
+                put_pair(weights[c], w_hi, w_lo, False, some)
 
         def query_part(c, part):
             if plan[c][1] == LANES:
@@ -235,7 +262,6 @@
                 table = tgt_ref[:, cols]
                 state = trow_ref[cols].reshape(1, width)
             else:
-                row_hop(bucket - 1, c).wait_recv()
                 table = recv[c][bucket - 1]
                 state = row_recv[bucket - 1, c, :, :width]
             if width == LANES:
@@ -250,8 +276,6 @@
             else:
                 send[c][bucket] = new
                 row_send[bucket, c, :, :width] = fresh
-                hop(bucket, c).start()
-                row_hop(bucket, c).start()
 
         def relate(part, whole):
             g_hi, g_lo = split(whole * picked[part, :])
@@ -261,27 +285,59 @@
             else:
                 rel_all[my_rel, part, :] = rel_all[my_rel, part, :] + rel_grad
 
-        if bucket == 0:
-            load_tgt.wait()
-            for copy in load_late:
-                copy.wait()
-            pl.semaphore_wait(barrier, n_rel)
         everything = pl.ds(0, dims)
+
+        def arrive(c):
+            if bucket > 0:
+                hop(bucket - 1, c).wait_recv()
+                row_hop(bucket - 1, c).wait_recv()
+
+        def depart(c):
+            hop(bucket, c).start()
+            row_hop(bucket, c).start()
+
         if not last:
-            for c in range(len(plan)):
-                weigh(c)
+            arrive(0)
+            weigh(0)
+            if bucket == 0:
+                load_late[0].wait()
+            finish(0)
+            if bucket == 0:
+                pl.semaphore_wait(barrier, n_rel)
+            depart(0)
+            if bucket == 0:
+                for copy in load_tgt[1:] + load_late[1:]:
+                    copy.wait()
+            if final > 0:
+                arrive(1)
+                weigh(1)
+            for c in range(1, final + 1):
+                if c < final:
+                    arrive(c + 1)
                 finish(c)
+                if c < final:
+                    weigh(c + 1)
+                depart(c)
             total = query_part(0, everything)
             for c in range(1, len(plan)):
                 total += query_part(c, everything)
             gq_ref[...] = total
             relate(everything, total)
         else:
-            for c in range(final):
-                weigh(c)
+            def gather_query(c):
                 part = query_part(c, everything)
                 gq_ref[...] = part if c == 0 else gq_ref[...] + part
-                finish(c)
+
+            for c in range(final):
+                arrive(c)
+                weigh(c)
+                if c > 0:
+                    gather_query(c - 1)
+                    finish(c - 1)
+            if final > 0:
+                gather_query(final - 1)
+                finish(final - 1)
+            arrive(final)
             weigh(final)
             for b, (r, n) in enumerate(blocks):
                 part = pl.ds(r, n)
@@ -330,13 +386,13 @@
         rels = relation_ops.shape[1]
         buckets, edges = source_ids.shape
         plan = chunk_plan(rows)
-        blocks = row_blocks(dims)
+        arrivals, blocks = row_blocks(dims)
         chunks = len(plan)
         vmem = pl.BlockSpec(memory_space=pltpu.VMEM)
         shape = jax.ShapeDtypeStruct
         moves = [pltpu.VMEM((buckets - 1, dims, width), F32) for _, width in plan]
         out = pl.pallas_call(
-            functools.partial(kernel, n_blk, n_rel, plan, blocks),
+            functools.partial(kernel, n_blk, n_rel, plan, arrivals, blocks),
             out_shape=(
                 pltpu.VMEM((dims, rows), F32), pltpu.VMEM((1, rows), F32),
                 pltpu.VMEM((dims, rows), F32), pltpu.VMEM((1, rows), F32),
@@ -349,7 +405,7 @@
                 pltpu.VMEM((dims, rows), F32), pltpu.VMEM((rows,), F32),
                 pltpu.VMEM((dims, rels), F32), pltpu.VMEM((dims, rels), F32),
                 *[pltpu.VMEM(ids.shape, jnp.int32) for ids in (source_ids, relation_ids, target_ids, negative_ids)],
-                pltpu.SemaphoreType.DMA((9 + len(blocks),)),
+                pltpu.SemaphoreType.DMA((10 + len(arrivals),)),
                 pltpu.VMEM((rows, edges), BF16),
                 pltpu.VMEM((rels, edges), BF16),
                 pltpu.VMEM((2, edges, dims), BF16),
@@ -357,6 +413,7 @@
                 pltpu.VMEM((dims, edges), F32),
                 pltpu.VMEM((dims, edges), F32),
                 pltpu.VMEM((dims, edges), F32),
+                pltpu.VMEM((1, rows), F32),
                 pltpu.VMEM((n_rel, dims, rels), F32),
                 pltpu.SemaphoreType.DMA((n_rel, len(blocks))),
                 pltpu.SemaphoreType.DMA((n_rel, len(blocks))),

time: 33.1 us -> 32.6 us (0.985)
  Pallas kernels: 32.3 us -> 31.8 us
    pallas_call x1, Pallas kernels: 30.7 us -> 30.2 us  [per_device(): pl.pallas_call(functools.partial(kernel, n_blk, n_rel, plan, arrivals, bl...]
where the time goes in v2:
time: 32.6 us; the launch traced here: 32.4 us
  Pallas kernels  31.8 us (98%)
  between operations  0.64 us (2%)
    pallas_call x1, Pallas kernels, per_device(): pl.pallas_call(functools.partial(kernel, n_blk, n_rel, plan, arrivals, bl...  30.2 us
    pallas_call x1, Pallas kernels, per_device(): pl.pallas_call(emit, out_shape=(shape((dims, rows), F32), shape((rows,),...  1.62 us

profile of v2, /device:TPU:0, one launch (start us, length us, event | category | flops | bytes accessed | tf_op | source)
XLA Modules:
  0.0 32.4 jit_solution(5188617949450390857)
XLA Ops:
  0.6 30.2 %shard_map.145 = (f32[400,768]{1,0:T(8,128)S(1)}, f32[1,768]{1,0:T(1,128)S(1)}, f32[400,768]{1,0:T(8,128)S(1)}, f32[1,768]{1,0:T(1,128)S(1)}, f32[400,128]{1,0:T(8,128)S(1)}, /*index=5*/f32[400,128]{1,0:T(8,128)S(1)}) custom-call(f32[400,768]{1,0:T(8,128)} %refs_0_.1, f32[768]{0:T(1024)} %refs_1_.1, f32[400,768]{1,0:T(8,128)} %refs_2_.1, f32[768]{0:T(1024)} %refs_3_.1, ...), custom_call_target="tpu_custom_call" | custom-call | tf_op jit(solution)/shard_map/pallas_call | solution.py:394
  30.8 1.6 %shard_map.146 = (f32[400,768]{1,0:T(8,128)}, f32[768]{0:T(1024)}, f32[400,768]{1,0:T(8,128)}, f32[768]{0:T(1024)}, f32[400,128]{1,0:T(8,128)}, /*index=5*/f32[400,128]{1,0:T(8,128)}) custom-call(f32[400,768]{1,0:T(8,128)S(1)} %get-tuple-element.12.refs_0_, f32[1,768]{1,0:T(1,128)S(1)} %get-tuple-element.13.refs_1_, ...), custom_call_target="tpu_custom_call" | custom-call | tf_op jit(solution)/shard_map/pallas_call | solution.py:440

commit v3 on v2

--- a/solution.py
+++ b/solution.py
@@ -51,6 +51,20 @@
     else:
         widths = [LANES] * (rows // LANES)
     return [(sum(widths[:i]), w) for i, w in enumerate(widths)]
+
+
+def piece_plan(plan, dims, n_blk):
+    half, quarter = (dims // 2 + 15) // 16 * 16, (dims // 4 + 15) // 16 * 16
+    relays = n_blk >= 16 and len(plan) > 2
+    pieces = []
+    for c in range(len(plan)):
+        if relays and c == 0:
+            pieces += [(c, 0, half, n_blk - 4), (c, half, dims - half, n_blk - 8)]
+        elif relays and c == 1:
+            pieces += [(c, 0, quarter, n_blk - 12), (c, quarter, dims - quarter, None)]
+        else:
+            pieces += [(c, 0, dims, None)]
+    return pieces
 
 
 def row_blocks(dims):
@@ -88,7 +102,7 @@
         copy.wait()
 
 
-def kernel(n_blk, n_rel, plan, arrivals, blocks, *refs):
+def kernel(n_blk, n_rel, plan, pieces, arrivals, blocks, *refs):
     refs = list(refs)
 
     def take(n):
@@ -103,6 +117,9 @@
     rsend_sem, rrecv_sem, send_sem, recv_sem, row_send, row_recv = take(6)
     tables, weights = take(len(plan)), take(len(plan))
     send, recv = take(len(plan)), take(len(plan))
+    relayed = [p for p, piece in enumerate(pieces) if piece[3] is not None]
+    relay_refs = dict(zip(relayed, take(len(relayed))))
+    relay_recv, relay_send, row_send_sem, row_recv_sem = take(4)
     dims, rows = src_ref.shape
     buckets, edges = sid_ref.shape
     negs = nid_ref.shape[1]
@@ -139,22 +156,68 @@
             barrier, inc=1, device_id={"rel": lax.rem(my_rel + step, n_rel)}, device_id_type=MESH
         )
 
-    def hop(bucket, c):
+    for p in relayed:
+        at = pieces[p][3]
+
+        @pl.when(my_blk == 0)
+        def _():
+            pl.semaphore_signal(barrier, inc=1, device_id={"blk": jnp.int32(at)}, device_id_type=MESH)
+
+        @pl.when(my_blk == at)
+        def _():
+            pl.semaphore_signal(barrier, inc=1, device_id={"blk": n_blk - 1}, device_id_type=MESH)
+
+    def enter():
+        expected = jnp.int32(n_rel)
+        for p in relayed:
+            expected += (my_blk == n_blk - 1).astype(jnp.int32) + (my_blk == pieces[p][3]).astype(jnp.int32)
+        pl.semaphore_wait(barrier, expected)
+
+    def hop(bucket, p):
+        c, r, n, _ = pieces[p]
         return pltpu.make_async_remote_copy(
-            src_ref=send[c].at[bucket],
-            dst_ref=recv[c].at[bucket],
-            send_sem=send_sem.at[0, bucket, c],
-            recv_sem=recv_sem.at[0, bucket, c],
+            src_ref=send[c].at[bucket, pl.ds(r, n)],
+            dst_ref=recv[c].at[bucket, pl.ds(r, n)],
+            send_sem=send_sem.at[bucket, p],
+            recv_sem=recv_sem.at[bucket, p],
             device_id={"blk": nxt},
             device_id_type=MESH,
         )
+
+    def to_relay(bucket, p):
+        c, r, n, at = pieces[p]
+        return pltpu.make_async_remote_copy(
+            src_ref=send[c].at[bucket, pl.ds(r, n)],
+            dst_ref=relay_refs[p].at[bucket],
+            send_sem=send_sem.at[bucket, p],
+            recv_sem=relay_recv.at[bucket, p],
+            device_id={"blk": jnp.int32(at)},
+            device_id_type=MESH,
+        )
+
+    def from_relay(bucket, p):
+        c, r, n, _ = pieces[p]
+        return pltpu.make_async_remote_copy(
+            src_ref=relay_refs[p].at[bucket],
+            dst_ref=recv[c].at[bucket, pl.ds(r, n)],
+            send_sem=relay_send.at[bucket, p],
+            recv_sem=recv_sem.at[bucket, p],
+            device_id={"blk": jnp.int32(0)},
+            device_id_type=MESH,
+        )
+
+    def relay(bucket, p):
+        @pl.when(my_blk == pieces[p][3])
+        def _():
+            to_relay(bucket, p).wait_recv()
+            from_relay(bucket, p).start()
 
     def row_hop(bucket, c):
         return pltpu.make_async_remote_copy(
             src_ref=row_send.at[bucket, c, :, pl.ds(0, plan[c][1])],
             dst_ref=row_recv.at[bucket, c, :, pl.ds(0, plan[c][1])],
-            send_sem=send_sem.at[1, bucket, c],
-            recv_sem=recv_sem.at[1, bucket, c],
+            send_sem=row_send_sem.at[bucket, c],
+            recv_sem=row_recv_sem.at[bucket, c],
             device_id={"blk": nxt},
             device_id_type=MESH,
         )
@@ -289,11 +352,25 @@
 
         def arrive(c):
             if bucket > 0:
-                hop(bucket - 1, c).wait_recv()
+                for p, piece in enumerate(pieces):
+                    if piece[0] == c:
+                        hop(bucket - 1, p).wait_recv()
                 row_hop(bucket - 1, c).wait_recv()
 
         def depart(c):
-            hop(bucket, c).start()
+            for p, piece in enumerate(pieces):
+                if piece[0] != c:
+                    continue
+                if p in relayed:
+                    @pl.when(my_blk == n_blk - 1)
+                    def _():
+                        to_relay(bucket, p).start()
+
+                    @pl.when(my_blk != n_blk - 1)
+                    def _():
+                        hop(bucket, p).start()
+                else:
+                    hop(bucket, p).start()
             row_hop(bucket, c).start()
 
         if not last:
@@ -303,7 +380,7 @@
                 load_late[0].wait()
             finish(0)
             if bucket == 0:
-                pl.semaphore_wait(barrier, n_rel)
+                enter()
             depart(0)
             if bucket == 0:
                 for copy in load_tgt[1:] + load_late[1:]:
@@ -318,6 +395,9 @@
                 if c < final:
                     weigh(c + 1)
                 depart(c)
+            for p in relayed:
+                if pieces[p][0] == 0:
+                    relay(bucket, p)
             total = query_part(0, everything)
             for c in range(1, len(plan)):
                 total += query_part(c, everything)
@@ -355,10 +435,19 @@
         fresh = now_srow + jnp.sum(src_grad * src_grad, axis=0, keepdims=True) * (1.0 / dims)
         out_src[...] = now_src[...] - src_grad * (learn_rate / (jnp.sqrt(fresh) + epsilon))
         out_srow[...] = fresh
+        if not last:
+            for p in relayed:
+                if pieces[p][0] > 0:
+                    relay(bucket, p)
 
     for bucket in range(buckets - 1):
+        for p in range(len(pieces)):
+            hop(bucket, p).wait_send()
+        for p in relayed:
+            @pl.when(my_blk == pieces[p][3])
+            def _():
+                from_relay(bucket, p).wait_send()
         for c in range(len(plan)):
-            hop(bucket, c).wait_send()
             row_hop(bucket, c).wait_send()
     for b, (r, n) in enumerate(blocks):
         part = pl.ds(r, n)
@@ -387,12 +476,13 @@
         buckets, edges = source_ids.shape
         plan = chunk_plan(rows)
         arrivals, blocks = row_blocks(dims)
+        pieces = piece_plan(plan, dims, n_blk)
         chunks = len(plan)
         vmem = pl.BlockSpec(memory_space=pltpu.VMEM)
         shape = jax.ShapeDtypeStruct
         moves = [pltpu.VMEM((buckets - 1, dims, width), F32) for _, width in plan]
         out = pl.pallas_call(
-            functools.partial(kernel, n_blk, n_rel, plan, arrivals, blocks),
+            functools.partial(kernel, n_blk, n_rel, plan, pieces, arrivals, blocks),
             out_shape=(
                 pltpu.VMEM((dims, rows), F32), pltpu.VMEM((1, rows), F32),
                 pltpu.VMEM((dims, rows), F32), pltpu.VMEM((1, rows), F32),
@@ -417,14 +507,22 @@
                 pltpu.VMEM((n_rel, dims, rels), F32),
                 pltpu.SemaphoreType.DMA((n_rel, len(blocks))),
                 pltpu.SemaphoreType.DMA((n_rel, len(blocks))),
-                pltpu.SemaphoreType.DMA((2, buckets - 1, chunks)),
-                pltpu.SemaphoreType.DMA((2, buckets - 1, chunks)),
+                pltpu.SemaphoreType.DMA((buckets - 1, len(pieces))),
+                pltpu.SemaphoreType.DMA((buckets - 1, len(pieces))),
                 pltpu.VMEM((buckets - 1, chunks, 1, 256), F32),
                 pltpu.VMEM((buckets - 1, chunks, 1, 256), F32),
                 *[pltpu.VMEM((2, dims, 256), BF16) for _ in plan],
                 *[pltpu.VMEM((2, edges, 256), BF16) for _ in plan],
                 *moves,
                 *moves,
+                *[
+                    pltpu.VMEM((buckets - 1, n, plan[c][1]), F32)
+                    for c, _, n, at in pieces if at is not None
+                ],
+                pltpu.SemaphoreType.DMA((buckets - 1, len(pieces))),
+                pltpu.SemaphoreType.DMA((buckets - 1, len(pieces))),
+                pltpu.SemaphoreType.DMA((buckets - 1, chunks)),
+                pltpu.SemaphoreType.DMA((buckets - 1, chunks)),
             ],
             compiler_params=pltpu.CompilerParams(
                 collective_id=0, has_side_effects=True, vmem_limit_bytes=40 * 1024 * 1024

time: 32.6 us -> 40.7 us (1.25)
  Pallas kernels: 31.8 us -> 39.9 us
    pallas_call x1, Pallas kernels: 30.2 us -> 38.3 us  [per_device(): pl.pallas_call(functools.partial(kernel, n_blk, n_rel, plan, pieces, arri...]
where the time goes in v3:
time: 40.7 us; the launch traced here: 40.6 us
  Pallas kernels  39.9 us (98%)
  between operations  0.64 us (2%)
    pallas_call x1, Pallas kernels, per_device(): pl.pallas_call(functools.partial(kernel, n_blk, n_rel, plan, pieces, arri...  38.3 us
    pallas_call x1, Pallas kernels, per_device(): pl.pallas_call(emit, out_shape=(shape((dims, rows), F32), shape((rows,),...  1.62 us

profile of v3, /device:TPU:0, one launch (start us, length us, event | category | flops | bytes accessed | tf_op | source)
XLA Modules:
  0.0 40.6 jit_solution(16684226525038268979)
XLA Ops:
  0.6 38.3 %shard_map.145 = (f32[400,768]{1,0:T(8,128)S(1)}, f32[1,768]{1,0:T(1,128)S(1)}, f32[400,768]{1,0:T(8,128)S(1)}, f32[1,768]{1,0:T(1,128)S(1)}, f32[400,128]{1,0:T(8,128)S(1)}, /*index=5*/f32[400,128]{1,0:T(8,128)S(1)}) custom-call(f32[400,768]{1,0:T(8,128)} %refs_0_.1, f32[768]{0:T(1024)} %refs_1_.1, f32[400,768]{1,0:T(8,128)} %refs_2_.1, f32[768]{0:T(1024)} %refs_3_.1, ...), custom_call_target="tpu_custom_call" | custom-call | tf_op jit(solution)/shard_map/pallas_call | solution.py:484
  38.9 1.6 %shard_map.146 = (f32[400,768]{1,0:T(8,128)}, f32[768]{0:T(1024)}, f32[400,768]{1,0:T(8,128)}, f32[768]{0:T(1024)}, f32[400,128]{1,0:T(8,128)}, /*index=5*/f32[400,128]{1,0:T(8,128)}) custom-call(f32[400,768]{1,0:T(8,128)S(1)} %get-tuple-element.12.refs_0_, f32[1,768]{1,0:T(1,128)S(1)} %get-tuple-element.13.refs_1_, ...), custom_call_target="tpu_custom_call" | custom-call | tf_op jit(solution)/shard_map/pallas_call | solution.py:538

commit v4 on v3

--- a/solution.py
+++ b/solution.py
@@ -54,14 +54,16 @@
 
 
 def piece_plan(plan, dims, n_blk):
-    half, quarter = (dims // 2 + 15) // 16 * 16, (dims // 4 + 15) // 16 * 16
+    half, eighth = (dims // 2 + 15) // 16 * 16, dims // 128 * 16
     relays = n_blk >= 16 and len(plan) > 2
     pieces = []
     for c in range(len(plan)):
         if relays and c == 0:
-            pieces += [(c, 0, half, n_blk - 4), (c, half, dims - half, n_blk - 8)]
+            pieces += [(c, 0, half, n_blk - 8), (c, half, dims - half, n_blk - 12)]
         elif relays and c == 1:
-            pieces += [(c, 0, quarter, n_blk - 12), (c, quarter, dims - quarter, None)]
+            pieces += [
+                (c, 0, eighth, n_blk - 8), (c, eighth, eighth, n_blk - 12), (c, 2 * eighth, dims - 2 * eighth, None)
+            ]
         else:
             pieces += [(c, 0, dims, None)]
     return pieces
@@ -118,6 +120,7 @@
     tables, weights = take(len(plan)), take(len(plan))
     send, recv = take(len(plan)), take(len(plan))
     relayed = [p for p, piece in enumerate(pieces) if piece[3] is not None]
+    helpers = sorted({pieces[p][3] for p in relayed})
     relay_refs = dict(zip(relayed, take(len(relayed))))
     relay_recv, relay_send, row_send_sem, row_recv_sem = take(4)
     dims, rows = src_ref.shape
@@ -156,9 +159,7 @@
             barrier, inc=1, device_id={"rel": lax.rem(my_rel + step, n_rel)}, device_id_type=MESH
         )
 
-    for p in relayed:
-        at = pieces[p][3]
-
+    for at in helpers:
         @pl.when(my_blk == 0)
         def _():
             pl.semaphore_signal(barrier, inc=1, device_id={"blk": jnp.int32(at)}, device_id_type=MESH)
@@ -169,8 +170,8 @@
 
     def enter():
         expected = jnp.int32(n_rel)
-        for p in relayed:
-            expected += (my_blk == n_blk - 1).astype(jnp.int32) + (my_blk == pieces[p][3]).astype(jnp.int32)
+        for at in helpers:
+            expected += (my_blk == n_blk - 1).astype(jnp.int32) + (my_blk == at).astype(jnp.int32)
         pl.semaphore_wait(barrier, expected)
 
     def hop(bucket, p):

time: 40.7 us -> 33.1 us (0.81)
  Pallas kernels: 39.9 us -> 32.2 us
    pallas_call x1, Pallas kernels: 38.3 us -> 30.6 us  [per_device(): pl.pallas_call(functools.partial(kernel, n_blk, n_rel, plan, pieces, arri...]
where the time goes in v4:
time: 33.1 us; the launch traced here: 32.9 us
  Pallas kernels  32.2 us (97%)
  between operations  0.64 us (2%)
    pallas_call x1, Pallas kernels, per_device(): pl.pallas_call(functools.partial(kernel, n_blk, n_rel, plan, pieces, arri...  30.6 us
    pallas_call x1, Pallas kernels, per_device(): pl.pallas_call(emit, out_shape=(shape((dims, rows), F32), shape((rows,),...  1.62 us

profile of v4, /device:TPU:0, one launch (start us, length us, event | category | flops | bytes accessed | tf_op | source)
XLA Modules:
  0.0 32.9 jit_solution(17145854198374213482)
XLA Ops:
  0.6 30.6 %shard_map.145 = (f32[400,768]{1,0:T(8,128)S(1)}, f32[1,768]{1,0:T(1,128)S(1)}, f32[400,768]{1,0:T(8,128)S(1)}, f32[1,768]{1,0:T(1,128)S(1)}, f32[400,128]{1,0:T(8,128)S(1)}, /*index=5*/f32[400,128]{1,0:T(8,128)S(1)}) custom-call(f32[400,768]{1,0:T(8,128)} %refs_0_.1, f32[768]{0:T(1024)} %refs_1_.1, f32[400,768]{1,0:T(8,128)} %refs_2_.1, f32[768]{0:T(1024)} %refs_3_.1, ...), custom_call_target="tpu_custom_call" | custom-call | tf_op jit(solution)/shard_map/pallas_call | solution.py:485
  31.3 1.6 %shard_map.146 = (f32[400,768]{1,0:T(8,128)}, f32[768]{0:T(1024)}, f32[400,768]{1,0:T(8,128)}, f32[768]{0:T(1024)}, f32[400,128]{1,0:T(8,128)}, /*index=5*/f32[400,128]{1,0:T(8,128)}) custom-call(f32[400,768]{1,0:T(8,128)S(1)} %get-tuple-element.12.refs_0_, f32[1,768]{1,0:T(1,128)S(1)} %get-tuple-element.13.refs_1_, ...), custom_call_target="tpu_custom_call" | custom-call | tf_op jit(solution)/shard_map/pallas_call | solution.py:539

commit v5 on v2

--- a/solution.py
+++ b/solution.py
@@ -54,9 +54,9 @@
 
 
 def row_blocks(dims):
-    first = min(256, dims // 16 * 16)
-    half = (dims // 2 + 15) // 16 * 16
-    return [(0, first), (first, dims - first)], [(0, half), (half, dims - half)]
+    first = dims // 64 * 16
+    second = first + (dims - first + 31) // 32 * 16
+    return [(0, first), (first, second - first), (second, dims - second)]
 
 
 def lane_gather(table, index):
@@ -88,7 +88,7 @@
         copy.wait()
 
 
-def kernel(n_blk, n_rel, plan, arrivals, blocks, *refs):
+def kernel(n_blk, n_rel, plan, blocks, *refs):
     refs = list(refs)
 
     def take(n):
@@ -101,6 +101,7 @@
     src_ref, srow_ref, tgt_ref, trow_ref, rel_ref, rstate_ref, sid_ref, rid_ref, tid_ref, nid_ref = take(10)
     load_sem, hot, rhot, qt_ref, q_ref, picked, relation, gq_ref, counts, rel_all = take(10)
     rsend_sem, rrecv_sem, send_sem, recv_sem, row_send, row_recv = take(6)
+    (turned,) = take(1)
     tables, weights = take(len(plan)), take(len(plan))
     send, recv = take(len(plan)), take(len(plan))
     dims, rows = src_ref.shape
@@ -125,7 +126,7 @@
         load(sid_in, sid_ref), load(rid_in, rid_ref), load(nid_in, nid_ref), load(tid_in, tid_ref)
     ]
     load_rel = load(rel_in, rel_ref)
-    load_src = [load(src_in.at[pl.ds(r, n)], src_ref.at[pl.ds(r, n)]) for r, n in arrivals]
+    load_src = load(src_in, src_ref)
     load_tgt = [
         load(tgt_in.at[:, pl.ds(start, width)], tgt_ref.at[:, pl.ds(start, width)])
         for start, width in ((0, plan[0][1]), (plan[0][1], rows - plan[0][1])) if width
@@ -193,34 +194,52 @@
         now_src = src_ref if bucket == 0 else out_src
         sid = sid_ref[pl.ds(bucket, 1), :]
         rid = rid_ref[pl.ds(bucket, 1), :]
+        hot[...] = one_hot(sid, rows)
         if bucket == 0:
             load_rel.wait()
-        hot[...] = one_hot(sid, rows)
-        nid = column(nid_ref[pl.ds(bucket, 1), :])
-        tid = column(tid_ref[pl.ds(bucket, 1), :])
-        for start in range(0, rows, LANES):
-            lane = lax.broadcasted_iota(jnp.int32, (negs, LANES), 1) + start
-            counts[:, pl.ds(start, LANES)] = jnp.sum(
-                (lane == nid).astype(F32), axis=0, keepdims=True
-            ) * (0.5 / negs)
-        relation[...] = lane_gather(rel_ref[...], rid)
-        if bucket == 0:
-            for copy in load_src + load_tgt[:1]:
+            for copy in (load_src, load_tgt[0], load_late[0]):
                 copy.wait()
         s_hi, s_lo = split(now_src[...])
         for e, m in groups:
             some = pl.ds(e, m)
             picked[:, some] = nn(s_hi, hot[:, some]) + nn(s_lo, hot[:, some])
+        relation[...] = lane_gather(rel_ref[...], rid)
         for e, m in groups:
             some = pl.ds(e, m)
-            queries = picked[:, some] * relation[:, some]
-            hi, lo = split(jnp.transpose(queries * 0.5))
-            qt_ref[0, some, :] = hi
-            qt_ref[1, some, :] = lo
-            hi, lo = split(queries)
+            hi, lo = split(picked[:, some] * relation[:, some])
             q_ref[0, :, some] = hi
             q_ref[1, :, some] = lo
-        rhot[...] = one_hot(rid, rels)
+
+        def turn():
+            for e, m in groups:
+                some = pl.ds(e, m)
+                hi, lo = split(jnp.transpose(picked[:, some] * relation[:, some] * 0.5))
+                qt_ref[0, some, :] = hi
+                qt_ref[1, some, :] = lo
+            nid = column(nid_ref[pl.ds(bucket, 1), :])
+            for start in range(0, rows, LANES):
+                lane = lax.broadcasted_iota(jnp.int32, (negs, LANES), 1) + start
+                counts[:, pl.ds(start, LANES)] = jnp.sum(
+                    (lane == nid).astype(F32), axis=0, keepdims=True
+                ) * (0.5 / negs)
+            rhot[...] = one_hot(rid, rels)
+            return column(tid_ref[pl.ds(bucket, 1), :])
+
+        def weigh_turned():
+            table = tgt_ref[:, :LANES]
+            hi, lo = split(table)
+            put_pair(tables[0], hi, lo, True)
+            hi, lo = split(jnp.transpose(table) * 0.5)
+            wide = nn(jnp.concatenate([hi, lo], axis=0), q_ref[0])
+            score = wide[:LANES] + wide[LANES:] + nn(hi, q_ref[1])
+            half = jnp.tanh(score)
+            here = lax.broadcasted_iota(jnp.int32, (LANES, negs), 0) == nid_ref[pl.ds(bucket, 1), :]
+            count = jnp.sum(here.astype(F32), axis=1, keepdims=True) * (0.5 / negs)
+            here = lax.broadcasted_iota(jnp.int32, (LANES, edges), 0) == tid_ref[pl.ds(bucket, 1), :]
+            weight = count * half + count - jnp.where(here, 0.5 - 0.5 * half, 0.0)
+            hi, lo = split(weight)
+            turned[:LANES, :] = hi
+            turned[LANES:, :] = lo
 
         def weigh(c):
             start, width = plan[c]
@@ -244,6 +263,8 @@
                 put_pair(weights[c], w_hi, w_lo, False, some)
 
         def query_part(c, part):
+            if bucket == 0 and c == 0:
+                return nn(tables[c][1, part, :], turned[...]) + nn(tables[c][0, part, LANES:], turned[:LANES, :])
             if plan[c][1] == LANES:
                 return (
                     nt(tables[c][1, part, :], weights[c][0])
@@ -264,7 +285,9 @@
             else:
                 table = recv[c][bucket - 1]
                 state = row_recv[bucket - 1, c, :, :width]
-            if width == LANES:
+            if bucket == 0 and c == 0:
+                grad = fold(nt(q_ref[0], turned[...])) + nt(q_ref[1], turned[:LANES, :])
+            elif width == LANES:
                 grad = fold(nn(q_ref[0], weights[c][0])) + nn(q_ref[1], weights[c][0, :, :LANES])
             else:
                 grad = nn(q_ref[0], weights[c][0]) + nn(q_ref[0], weights[c][1]) + nn(q_ref[1], weights[c][0])
@@ -297,17 +320,20 @@
             row_hop(bucket, c).start()
 
         if not last:
-            arrive(0)
-            weigh(0)
             if bucket == 0:
-                load_late[0].wait()
-            finish(0)
-            if bucket == 0:
+                weigh_turned()
+                finish(0)
                 pl.semaphore_wait(barrier, n_rel)
-            depart(0)
-            if bucket == 0:
+                depart(0)
                 for copy in load_tgt[1:] + load_late[1:]:
                     copy.wait()
+                tid = turn()
+            else:
+                tid = turn()
+                arrive(0)
+                weigh(0)
+                finish(0)
+                depart(0)
             if final > 0:
                 arrive(1)
                 weigh(1)
@@ -315,9 +341,12 @@
                 if c < final:
                     arrive(c + 1)
                 finish(c)
+                if c == 1:
+                    depart(c)
                 if c < final:
                     weigh(c + 1)
-                depart(c)
+                if c > 1:
+                    depart(c)
             total = query_part(0, everything)
             for c in range(1, len(plan)):
                 total += query_part(c, everything)
@@ -328,9 +357,14 @@
                 part = query_part(c, everything)
                 gq_ref[...] = part if c == 0 else gq_ref[...] + part
 
+            tid = turn()
+            if bucket == 0:
+                pl.semaphore_wait(barrier, n_rel)
+                for copy in load_tgt[1:] + load_late[1:]:
+                    copy.wait()
             for c in range(final):
                 arrive(c)
-                weigh(c)
+                weigh_turned() if bucket == 0 and c == 0 else weigh(c)
                 if c > 0:
                     gather_query(c - 1)
                     finish(c - 1)
@@ -386,13 +420,13 @@
         rels = relation_ops.shape[1]
         buckets, edges = source_ids.shape
         plan = chunk_plan(rows)
-        arrivals, blocks = row_blocks(dims)
+        blocks = row_blocks(dims)
         chunks = len(plan)
         vmem = pl.BlockSpec(memory_space=pltpu.VMEM)
         shape = jax.ShapeDtypeStruct
         moves = [pltpu.VMEM((buckets - 1, dims, width), F32) for _, width in plan]
         out = pl.pallas_call(
-            functools.partial(kernel, n_blk, n_rel, plan, arrivals, blocks),
+            functools.partial(kernel, n_blk, n_rel, plan, blocks),
             out_shape=(
                 pltpu.VMEM((dims, rows), F32), pltpu.VMEM((1, rows), F32),
                 pltpu.VMEM((dims, rows), F32), pltpu.VMEM((1, rows), F32),
@@ -405,7 +439,7 @@
                 pltpu.VMEM((dims, rows), F32), pltpu.VMEM((rows,), F32),
                 pltpu.VMEM((dims, rels), F32), pltpu.VMEM((dims, rels), F32),
                 *[pltpu.VMEM(ids.shape, jnp.int32) for ids in (source_ids, relation_ids, target_ids, negative_ids)],
-                pltpu.SemaphoreType.DMA((10 + len(arrivals),)),
+                pltpu.SemaphoreType.DMA((11,)),
                 pltpu.VMEM((rows, edges), BF16),
                 pltpu.VMEM((rels, edges), BF16),
                 pltpu.VMEM((2, edges, dims), BF16),
@@ -421,6 +455,7 @@
                 pltpu.SemaphoreType.DMA((2, buckets - 1, chunks)),
                 pltpu.VMEM((buckets - 1, chunks, 1, 256), F32),
                 pltpu.VMEM((buckets - 1, chunks, 1, 256), F32),
+                pltpu.VMEM((2 * LANES, edges), BF16),
                 *[pltpu.VMEM((2, dims, 256), BF16) for _ in plan],
                 *[pltpu.VMEM((2, edges, 256), BF16) for _ in plan],
                 *moves,

time: 32.6 us -> 32.2 us (0.988)
  Pallas kernels: 31.8 us -> 31.3 us
    pallas_call x1, Pallas kernels: 30.2 us -> 29.7 us  [per_device(): pl.pallas_call(functools.partial(kernel, n_blk, n_rel, plan, blocks), out...]
where the time goes in v5:
time: 32.2 us; the launch traced here: 32 us
  Pallas kernels  31.3 us (97%)
  between operations  0.64 us (2%)
    pallas_call x1, Pallas kernels, per_device(): pl.pallas_call(functools.partial(kernel, n_blk, n_rel, plan, blocks), out...  29.7 us
    pallas_call x1, Pallas kernels, per_device(): pl.pallas_call(emit, out_shape=(shape((dims, rows), F32), shape((rows,),...  1.62 us

profile of v5, /device:TPU:0, one launch (start us, length us, event | category | flops | bytes accessed | tf_op | source)
XLA Modules:
  0.0 32.0 jit_solution(18338402737653124008)
XLA Ops:
  0.6 29.7 %shard_map.145 = (f32[400,768]{1,0:T(8,128)S(1)}, f32[1,768]{1,0:T(1,128)S(1)}, f32[400,768]{1,0:T(8,128)S(1)}, f32[1,768]{1,0:T(1,128)S(1)}, f32[400,128]{1,0:T(8,128)S(1)}, /*index=5*/f32[400,128]{1,0:T(8,128)S(1)}) custom-call(f32[400,768]{1,0:T(8,128)} %refs_0_.1, f32[768]{0:T(1024)} %refs_1_.1, f32[400,768]{1,0:T(8,128)} %refs_2_.1, f32[768]{0:T(1024)} %refs_3_.1, ...), custom_call_target="tpu_custom_call" | custom-call | tf_op jit(solution)/shard_map/pallas_call | solution.py:428
  30.4 1.6 %shard_map.146 = (f32[400,768]{1,0:T(8,128)}, f32[768]{0:T(1024)}, f32[400,768]{1,0:T(8,128)}, f32[768]{0:T(1024)}, f32[400,128]{1,0:T(8,128)}, /*index=5*/f32[400,128]{1,0:T(8,128)}) custom-call(f32[400,768]{1,0:T(8,128)S(1)} %get-tuple-element.12.refs_0_, f32[1,768]{1,0:T(1,128)S(1)} %get-tuple-element.13.refs_1_, ...), custom_call_target="tpu_custom_call" | custom-call | tf_op jit(solution)/shard_map/pallas_call | solution.py:475

commit v6 on v5

--- a/solution.py
+++ b/solution.py
@@ -125,8 +125,15 @@
     load_ids = [
         load(sid_in, sid_ref), load(rid_in, rid_ref), load(nid_in, nid_ref), load(tid_in, tid_ref)
     ]
+    quarter = dims // 64 * 16
+    ends = [0, quarter, 2 * quarter, 3 * quarter, dims]
+    load_src = [
+        load(src_in.at[pl.ds(r, n - r)], src_ref.at[pl.ds(r, n - r)]) for r, n in zip(ends[:2], ends[1:3])
+    ]
     load_rel = load(rel_in, rel_ref)
-    load_src = load(src_in, src_ref)
+    load_src += [
+        load(src_in.at[pl.ds(r, n - r)], src_ref.at[pl.ds(r, n - r)]) for r, n in zip(ends[2:4], ends[3:])
+    ]
     load_tgt = [
         load(tgt_in.at[:, pl.ds(start, width)], tgt_ref.at[:, pl.ds(start, width)])
         for start, width in ((0, plan[0][1]), (plan[0][1], rows - plan[0][1])) if width
@@ -195,14 +202,18 @@
         sid = sid_ref[pl.ds(bucket, 1), :]
         rid = rid_ref[pl.ds(bucket, 1), :]
         hot[...] = one_hot(sid, rows)
-        if bucket == 0:
-            load_rel.wait()
-            for copy in (load_src, load_tgt[0], load_late[0]):
-                copy.wait()
-        s_hi, s_lo = split(now_src[...])
-        for e, m in groups:
-            some = pl.ds(e, m)
-            picked[:, some] = nn(s_hi, hot[:, some]) + nn(s_lo, hot[:, some])
+        for first in (0, 2):
+            part = pl.ds(ends[first], ends[first + 2] - ends[first])
+            if bucket == 0:
+                for copy in load_src[first:first + 2]:
+                    copy.wait()
+                if first:
+                    for copy in (load_rel, load_tgt[0], load_late[0]):
+                        copy.wait()
+            s_hi, s_lo = split(now_src[part, :])
+            for e, m in groups:
+                some = pl.ds(e, m)
+                picked[part, some] = nn(s_hi, hot[:, some]) + nn(s_lo, hot[:, some])
         relation[...] = lane_gather(rel_ref[...], rid)
         for e, m in groups:
             some = pl.ds(e, m)
@@ -262,18 +273,21 @@
                 w_hi, w_lo = split(weight)
                 put_pair(weights[c], w_hi, w_lo, False, some)
 
-        def query_part(c, part):
+        def query_part(c, part, some=slice(None)):
             if bucket == 0 and c == 0:
-                return nn(tables[c][1, part, :], turned[...]) + nn(tables[c][0, part, LANES:], turned[:LANES, :])
+                return (
+                    nn(tables[c][1, part, :], turned[:, some])
+                    + nn(tables[c][0, part, LANES:], turned[:LANES, some])
+                )
             if plan[c][1] == LANES:
                 return (
-                    nt(tables[c][1, part, :], weights[c][0])
-                    + nt(tables[c][0, part, LANES:], weights[c][0, :, :LANES])
+                    nt(tables[c][1, part, :], weights[c][0, some, :])
+                    + nt(tables[c][0, part, LANES:], weights[c][0, some, :LANES])
                 )
             return (
-                nt(tables[c][0, part, :], weights[c][0])
-                + nt(tables[c][0, part, :], weights[c][1])
-                + nt(tables[c][1, part, :], weights[c][0])
+                nt(tables[c][0, part, :], weights[c][0, some, :])
+                + nt(tables[c][0, part, :], weights[c][1, some, :])
+                + nt(tables[c][1, part, :], weights[c][0, some, :])
             )
 
         def finish(c):
@@ -375,11 +389,16 @@
             weigh(final)
             for b, (r, n) in enumerate(blocks):
                 part = pl.ds(r, n)
-                whole = query_part(final, part)
-                if final > 0:
-                    whole = gq_ref[part, :] + whole
-                gq_ref[part, :] = whole
-                relate(part, whole)
+                rel_grad = rel_all[my_rel, part, :] if bucket > 0 else 0.0
+                for e, m in groups:
+                    some = pl.ds(e, m)
+                    whole = query_part(final, part, some)
+                    if final > 0:
+                        whole = gq_ref[part, some] + whole
+                    gq_ref[part, some] = whole
+                    g_hi, g_lo = split(whole * picked[part, some])
+                    rel_grad += nt(g_hi, rhot[:, some]) + nt(g_lo, rhot[:, some])
+                rel_all[my_rel, part, :] = rel_grad
                 for step in range(1, n_rel):
                     rel_hop(lax.rem(my_rel + step, n_rel), my_rel, step, b).start()
             finish(final)
@@ -439,7 +458,7 @@
                 pltpu.VMEM((dims, rows), F32), pltpu.VMEM((rows,), F32),
                 pltpu.VMEM((dims, rels), F32), pltpu.VMEM((dims, rels), F32),
                 *[pltpu.VMEM(ids.shape, jnp.int32) for ids in (source_ids, relation_ids, target_ids, negative_ids)],
-                pltpu.SemaphoreType.DMA((11,)),
+                pltpu.SemaphoreType.DMA((14,)),
                 pltpu.VMEM((rows, edges), BF16),
                 pltpu.VMEM((rels, edges), BF16),
                 pltpu.VMEM((2, edges, dims), BF16),

time: 32.2 us -> 32.2 us (level)
  no operation moved by 1% of the time
where the time goes in v6:
time: 32.2 us; the launch traced here: 32 us
  Pallas kernels  31.3 us (97%)
  between operations  0.64 us (2%)
    pallas_call x1, Pallas kernels, per_device(): pl.pallas_call(functools.partial(kernel, n_blk, n_rel, plan, blocks), out...  29.7 us
    pallas_call x1, Pallas kernels, per_device(): pl.pallas_call(emit, out_shape=(shape((dims, rows), F32), shape((rows,),...  1.62 us

profile of v6, /device:TPU:0, one launch (start us, length us, event | category | flops | bytes accessed | tf_op | source)
XLA Modules:
  0.0 32.0 jit_solution(11811575587580838008)
XLA Ops:
  0.6 29.7 %shard_map.145 = (f32[400,768]{1,0:T(8,128)S(1)}, f32[1,768]{1,0:T(1,128)S(1)}, f32[400,768]{1,0:T(8,128)S(1)}, f32[1,768]{1,0:T(1,128)S(1)}, f32[400,128]{1,0:T(8,128)S(1)}, /*index=5*/f32[400,128]{1,0:T(8,128)S(1)}) custom-call(f32[400,768]{1,0:T(8,128)} %refs_0_.1, f32[768]{0:T(1024)} %refs_1_.1, f32[400,768]{1,0:T(8,128)} %refs_2_.1, f32[768]{0:T(1024)} %refs_3_.1, ...), custom_call_target="tpu_custom_call" | custom-call | tf_op jit(solution)/shard_map/pallas_call | solution.py:447
  30.4 1.6 %shard_map.146 = (f32[400,768]{1,0:T(8,128)}, f32[768]{0:T(1024)}, f32[400,768]{1,0:T(8,128)}, f32[768]{0:T(1024)}, f32[400,128]{1,0:T(8,128)}, /*index=5*/f32[400,128]{1,0:T(8,128)}) custom-call(f32[400,768]{1,0:T(8,128)S(1)} %get-tuple-element.12.refs_0_, f32[1,768]{1,0:T(1,128)S(1)} %get-tuple-element.13.refs_1_, ...), custom_call_target="tpu_custom_call" | custom-call | tf_op jit(solution)/shard_map/pallas_call | solution.py:494
